TPU v7x, 32 devices: a whole 2x2x4 slice. The times are simulated.
32 devices in a mesh: groups: 2 (over x), dp: 16 (over z, y, core).
Axes of the slice: x: 2, y: 2, z: 4, core: 2. Of those that a mesh axis runs over, the one named last changes fastest.
Arguments:
- queries: bfloat16 [24576, 4096], P(('groups', 'dp')), parts along dimension 0, may hold values from -120 to 120
- keys: bfloat16 [24576, 512], P(('groups', 'dp')), parts along dimension 0, may hold values from -6 to 6
- values: bfloat16 [24576, 512], P(('groups', 'dp')), parts along dimension 0, may hold values from -6 to 6
- block_counts: int32 [32], P(('groups', 'dp')), parts along dimension 0, may hold values from 0 to 6, as said below
- segment_ids: int32 [8192], P(('groups', 'dp')), parts along dimension 0, may hold values from 0 to 7, never falling along the last dimension, each value on 1 to 1024 neighbouring positions
- reward_dir: float32 [4096], replicated, may hold values from -4 to 4
Outputs:
- attn_out: bfloat16 [8192, 4096], P(('groups', 'dp')), parts along dimension 0
- rewards: float32 [16], P('groups'), parts along dimension 0
There are 2 independent parts, one for each index of `groups`. A program takes and returns all parts, laid end to end along the dimension named above; an argument that names none is the same for every part. Nothing has to cross between parts.
Inputs may be any that keep to these rules, and one draw needn't show every extreme that they name: `block_counts`: the counts sum to 2 times the number of ranks; for each rank s the counts of the ranks before s sum to between (2 * s - 2) and (2 * s + 2); some rank holds 6. `segment_ids`: positions never fall in segment number, each of the 8 responses holds 1 to 1024 positions.
All inputs are finite; a program needn't handle non-finite values.
Results may differ from a plain program's by a relative error of at most 0.0039.
The roundings to bfloat16 on the way count: a program that leaves them out, or rounds other values in their place, can miss the bound.
Values may be sent and summed in bfloat16 or wider, within the bound.
No kernel may reach another device: no remote copies, remote signals or barrier semaphores. Data moves between devices by JAX's collectives and lax.ppermute only.
A program may use at most 128 MiB of HBM per device.

v0:
```python
import jax
import jax.numpy as jnp
from jax import lax
from jax.sharding import PartitionSpec as P

D_HEAD = 128
HEADS = 32
KV_HEADS = 4
BLOCK = 128
RECV = 2
REACH = 4


def prefix_2(part, axis, combine, identity):
    place = lax.axis_index(axis)
    gathered = jax.tree.map(lambda a: lax.all_gather(a, axis), part)
    state = jax.tree.map(lambda a, e: jnp.zeros_like(a) + jnp.asarray(e, a.dtype), part, identity)

    def one(hop, state):
        return combine(
            state, jax.tree.map(lambda a: lax.dynamic_index_in_dim(a, hop, 0, False), gathered)
        )

    return lax.fori_loop(0, place, one, state)


def shifted(block, axis, distance):
    devices = range(lax.axis_size(axis))
    route = [(i - distance, i) for i in devices if i - distance in devices]
    return lax.ppermute(block, axis, route)


def shortened(shard):
    return jax.tree.map(lambda a: a.astype(jnp.bfloat16) if a.dtype == jnp.float32 else a, shard)


def attend(query_rows, key_window, value_window, allowed):
    per_group = HEADS // KV_HEADS
    row_count = query_rows.shape[0]
    score_scale = D_HEAD ** (-0.5)
    grouped = query_rows.reshape(row_count, KV_HEADS, per_group, D_HEAD)
    key_heads = key_window.reshape(-1, KV_HEADS, D_HEAD)
    value_heads = value_window.reshape(-1, KV_HEADS, D_HEAD)
    head_outs = []
    for head_index in range(KV_HEADS):
        query_head = grouped[:, head_index].reshape(row_count * per_group, D_HEAD)
        logits = (
            jnp.dot(query_head, key_heads[:, head_index].T, preferred_element_type=jnp.float32)
            * score_scale
        )
        logits = logits.reshape(row_count, per_group, -1)
        logits = jnp.where(allowed[:, None, :], logits, -1e30)
        row_max = jnp.max(logits, axis=-1, keepdims=True)
        raised = jnp.exp(logits - row_max)
        totals = jnp.sum(raised, axis=-1)
        soft_weights = raised.astype(jnp.bfloat16).reshape(row_count * per_group, -1)
        head_out = jnp.dot(
            soft_weights, value_heads[:, head_index], preferred_element_type=jnp.float32
        )
        head_out = head_out.reshape(row_count, per_group, D_HEAD) / totals[..., None]
        head_outs.append(head_out.astype(jnp.bfloat16))
    return jnp.stack(head_outs, axis=1).reshape(row_count, HEADS * D_HEAD)


def combine_all(earlier, later):
    count_a, first_a, last_a, start_a = earlier
    count_b, first_b, last_b, start_b = later
    joined = (first_b == last_b) & (last_a == first_b)
    empty_b = last_b < 0
    return (
        count_a + count_b,
        jnp.where(first_a < 0, first_b, first_a),
        jnp.where(empty_b, last_a, last_b),
        jnp.where(empty_b | joined, start_a, start_b),
    )


def shards(queries, keys, values, block_counts, segment_ids, reward_dir):
    row_count = segment_ids.shape[0]
    capacity = queries.shape[0] // BLOCK
    own_rank = lax.axis_index("dp")
    own_count = block_counts[0]
    positions = jnp.arange(row_count, dtype=jnp.int32)
    base_row = own_rank * row_count
    changed = jnp.concatenate([jnp.ones((1,), bool), segment_ids[1:] != segment_ids[:-1]])
    local_start = lax.cummax(jnp.where(changed, positions, 0), axis=0)
    summary = (
        block_counts,
        segment_ids[0:1],
        segment_ids[row_count - 1 : row_count],
        base_row + local_start[row_count - 1 : row_count],
    )
    neutral = (
        jnp.zeros((1,), jnp.int32),
        jnp.full((1,), -1, jnp.int32),
        jnp.full((1,), -1, jnp.int32),
        jnp.zeros((1,), jnp.int32),
    )
    prefix = prefix_2(summary, "dp", combine_all, neutral)
    offset = prefix[0][0]
    starts = jnp.where(segment_ids == prefix[2][0], prefix[3][0], base_row + local_start)
    following = shifted(segment_ids[0:1] + 1, "dp", -1)[0] - 1
    next_ids = jnp.concatenate([segment_ids[1:], following[None]])
    is_last = segment_ids != next_ids

    def outgoing(members, distance):
        first_pick = (own_rank + distance) * RECV - offset
        picks = first_pick + jnp.arange(RECV, dtype=jnp.int32)
        usable = (picks >= 0) & (picks < own_count)
        bounded = jnp.clip(picks, 0, capacity - 1)
        result = []
        for member in members:
            blocks = member.reshape(capacity, BLOCK, member.shape[1])
            chosen = jnp.take(blocks, bounded, axis=0)
            kept = jnp.where(usable[:, None, None], chosen, jnp.zeros_like(chosen))
            result.append(kept.reshape(row_count, member.shape[1]))
        return tuple(result)

    members = (queries, keys, values)
    arranged = outgoing(members, 0)
    for distance in (1, -1):
        parts = outgoing(members, distance)
        arrived = jax.tree.map(
            lambda part, own: part.astype(own.dtype),
            shifted(shortened(parts), "dp", distance),
            parts,
        )
        arranged = tuple((held + extra for held, extra in zip(arranged, arrived)))
    query_rows, key_rows, value_rows = arranged
    earlier = []
    carried = (key_rows, value_rows)
    for hop_index in range(REACH):
        carried = shifted((carried[0], carried[1]), "dp", 1)
        earlier.append(carried)
    earlier = earlier[::-1]
    key_window = jnp.concatenate([piece[0] for piece in earlier] + [key_rows], axis=0)
    value_window = jnp.concatenate([piece[1] for piece in earlier] + [value_rows], axis=0)
    key_window, value_window = (key_window, value_window)
    reach_rows = REACH * row_count
    key_pos = base_row - reach_rows + jnp.arange(reach_rows + row_count, dtype=jnp.int32)
    query_pos = base_row + positions
    allowed = (key_pos[None, :] >= starts[:, None]) & (key_pos[None, :] <= query_pos[:, None])
    attn_out = attend(query_rows, key_window, value_window, allowed)
    token_score = jnp.dot(attn_out.astype(jnp.float32), reward_dir, precision=lax.Precision.HIGHEST)
    response_count = lax.axis_size("dp") * 2 // REACH
    matches = (
        segment_ids[:, None] == jnp.arange(response_count, dtype=jnp.int32)[None, :]
    ) & is_last[:, None]
    partial_rewards = jnp.sum(jnp.where(matches, token_score[:, None], 0.0), axis=0)
    rewards = lax.psum(partial_rewards, "dp")
    return (attn_out, rewards)


def solution(mesh):
    return jax.shard_map(
        shards,
        mesh=mesh,
        in_specs=(
            P(("groups", "dp"), None),
            P(("groups", "dp"), None),
            P(("groups", "dp"), None),
            P(("groups", "dp")),
            P(("groups", "dp")),
            P(),
        ),
        out_specs=(P(("groups", "dp"), None), P("groups")),
        check_vma=False,
    )
```

profile of v0, /device:TPU:0, one launch (start us, length us, event | category | flops | bytes accessed | tf_op | source)
XLA Modules:
  0.0 308.4 jit_solution(2750992244555226999)
XLA Ops:
  2.0 1.9 fusion.63
  11.2 15.8 %all-reduce.4 = (s32[16]{0:T(128)S(1)}, s32[16]{0:T(128)S(1)}, s32[16]{0:T(128)S(1)}, s32[16]{0:T(128)S(1)}) all-reduce(s32[16]{0:T(128)S(1)} %dynamic-update-slice, s32[16]{0:T(128)S(1)} %slice_dynamic-update-slice_fusion, s32[16]{0:T(128)S(1)} %get-tuple-element.116, ...), channel_id=2, replica_groups=mesh['groups'=2,'dp'=16] {'dp'}, use_global_device_ids=true, to_apply=%add | all-reduce | flops 64 | bytes 512
  30.3 5.7 %collective-permute-start.2 = (bf16[256,512]{0,1:T(8,128)(2,1)}, bf16[256,512]{0,1:T(8,128)(2,1)}, u32[]{:S(2)}, u32[]{:S(2)}) collective-permute-start(bf16[256,512]{0,1:T(8,128)(2,1)} %copy.48), channel_id=1, source_target_pairs={{0,1},{1,2},{2,3},{3,4},{4,5},{5,6},{6,7},{7,8},{8,9},{9,10},{10,1... | collective-permute-start | bytes 786440 | tf_op jit(solution)/shard_map/ppermute | solution.py:30
  36.2 11.8 %collective-permute-start.8 = (bf16[256,512]{0,1:T(8,128)(2,1)S(1)}, bf16[256,512]{0,1:T(8,128)(2,1)}, u32[]{:S(2)}, u32[]{:S(2)}) collective-permute-start(bf16[256,512]{0,1:T(8,128)(2,1)S(1)} %copy.52), channel_id=1, source_target_pairs={{0,1},{1,2},{2,3},{3,4},{4,5},{5,6},{6,7},{7,8},{8,9},{9,10},{10,1... | collective-permute-start | bytes 786440 | tf_op jit(solution)/shard_map/ppermute | solution.py:30
  54.8 3.5 %gather_fusion.2 = bf16[2,128,4096]{2,1,0:T(8,128)(2,1)S(1)} fusion(bf16[6,128,4096]{2,1,0:T(8,128)(2,1)} %bitcast.181, s32[1024]{0:T(1024)S(1)} %get-tuple-element.133), kind=kCustom, calls=%fused_computation.3.clone | custom fusion | bytes 4194312 | tf_op jit(solution)/shard_map/jit(_take)/gather | solution.py:114
  62.2 3.5 %gather_fusion.1 = bf16[2,128,4096]{2,1,0:T(8,128)(2,1)S(1)} fusion(bf16[6,128,4096]{2,1,0:T(8,128)(2,1)} %bitcast.182, s32[1024]{0:T(1024)S(1)} %get-tuple-element.134), kind=kCustom, calls=%fused_computation.2.clone | custom fusion | bytes 4194312 | tf_op jit(solution)/shard_map/jit(_take)/gather | solution.py:114
  68.3 7.0 %collective-permute-start.10 = (bf16[256,512]{0,1:T(8,128)(2,1)S(1)}, bf16[256,512]{0,1:T(8,128)(2,1)S(1)}, u32[]{:S(2)}, u32[]{:S(2)}) collective-permute-start(bf16[256,512]{0,1:T(8,128)(2,1)S(1)} %add_add_fusion), channel_id=1, source_target_pairs={{0,1},{1,2},{2,3},{3,4},{4,5},{5,6},{6,7},{7,8},{8,9},{9,10},{10,1... | collective-permute-start | bytes 786440 | tf_op jit(solution)/shard_map/ppermute | solution.py:30
  76.9 3.5 %gather_fusion = bf16[2,128,4096]{2,1,0:T(8,128)(2,1)S(1)} fusion(bf16[6,128,4096]{2,1,0:T(8,128)(2,1)} %bitcast.183, s32[1024]{0:T(1024)S(1)} %pad_clamp_fusion.2), kind=kCustom, calls=%fused_computation.clone | custom fusion | bytes 4194312 | tf_op jit(solution)/shard_map/jit(_take)/gather | solution.py:114
  80.5 12.0 %collective-permute-start = (bf16[256,4096]{1,0:T(8,128)(2,1)}, bf16[256,4096]{1,0:T(8,128)(2,1)}, u32[]{:S(2)}, u32[]{:S(2)}) collective-permute-start(bf16[256,4096]{1,0:T(8,128)(2,1)} %bitcast.185), channel_id=1, source_target_pairs={{0,1},{1,2},{2,3},{3,4},{4,5},{5,6},{6,7},{7,8},{8,9},{9,10},{10,1... | collective-permute-start | bytes 6291464 | tf_op jit(solution)/shard_map/ppermute | solution.py:30
  93.5 4.9 %collective-permute-start.4 = (bf16[256,512]{0,1:T(8,128)(2,1)S(1)}, bf16[256,512]{0,1:T(8,128)(2,1)S(1)}, u32[]{:S(2)}, u32[]{:S(2)}) collective-permute-start(bf16[256,512]{0,1:T(8,128)(2,1)S(1)} %add_add_fusion.1), channel_id=1, source_target_pairs={{0,1},{1,2},{2,3},{3,4},{4,5},{5,6},{6,7},{7,8},{8,9},{9,10},{10,1... | collective-permute-start | bytes 786440 | tf_op jit(solution)/shard_map/ppermute | solution.py:30
  98.5 10.7 %collective-permute-start.11 = (bf16[256,512]{0,1:T(8,128)(2,1)S(1)}, bf16[256,512]{0,1:T(8,128)(2,1)S(1)}, u32[]{:S(2)}, u32[]{:S(2)}) collective-permute-start(bf16[256,512]{0,1:T(8,128)(2,1)S(1)} %collective-permute-done.10), channel_id=1, source_target_pairs={{0,1},{1,2},{2,3},{3,4},{4,5},{5,6},{6,7},{7,8},{8,9},{9,10},{10,1... | collective-permute-start | bytes 786440 | tf_op jit(solution)/shard_map/ppermute | solution.py:30
  110.8 32.0 %collective-permute-start.5 = (bf16[256,512]{0,1:T(8,128)(2,1)S(1)}, bf16[256,512]{0,1:T(8,128)(2,1)S(1)}, u32[]{:S(2)}, u32[]{:S(2)}) collective-permute-start(bf16[256,512]{0,1:T(8,128)(2,1)S(1)} %collective-permute-done.4), channel_id=1, source_target_pairs={{0,1},{1,2},{2,3},{3,4},{4,5},{5,6},{6,7},{7,8},{8,9},{9,10},{10,1... | collective-permute-start | bytes 786440 | tf_op jit(solution)/shard_map/ppermute | solution.py:30
  142.9 4.4 %collective-permute-start.12 = (bf16[256,512]{0,1:T(8,128)(2,1)S(1)}, bf16[256,512]{0,1:T(8,128)(2,1)S(1)}, u32[]{:S(2)}, u32[]{:S(2)}) collective-permute-start(bf16[256,512]{0,1:T(8,128)(2,1)S(1)} %collective-permute-done.11), channel_id=1, source_target_pairs={{0,1},{1,2},{2,3},{3,4},{4,5},{5,6},{6,7},{7,8},{8,9},{9,10},{10,1... | collective-permute-start | bytes 786440 | tf_op jit(solution)/shard_map/ppermute | solution.py:30
  147.3 3.2 %collective-permute-start.6 = (bf16[256,512]{0,1:T(8,128)(2,1)S(1)}, bf16[256,512]{0,1:T(8,128)(2,1)S(1)}, u32[]{:S(2)}, u32[]{:S(2)}) collective-permute-start(bf16[256,512]{0,1:T(8,128)(2,1)S(1)} %collective-permute-done.5), channel_id=1, source_target_pairs={{0,1},{1,2},{2,3},{3,4},{4,5},{5,6},{6,7},{7,8},{8,9},{9,10},{10,1... | collective-permute-start | bytes 786440 | tf_op jit(solution)/shard_map/ppermute | solution.py:30
  150.5 4.4 %collective-permute-start.13 = (bf16[256,512]{0,1:T(8,128)(2,1)S(1)}, bf16[256,512]{0,1:T(8,128)(2,1)S(1)}, u32[]{:S(2)}, u32[]{:S(2)}) collective-permute-start(bf16[256,512]{0,1:T(8,128)(2,1)S(1)} %collective-permute-done.12), channel_id=1, source_target_pairs={{0,1},{1,2},{2,3},{3,4},{4,5},{5,6},{6,7},{7,8},{8,9},{9,10},{10,1... | collective-permute-start | bytes 786440 | tf_op jit(solution)/shard_map/ppermute | solution.py:30
  156.1 21.6 %collective-permute-start.7 = (bf16[256,512]{0,1:T(8,128)(2,1)S(1)}, bf16[256,512]{0,1:T(8,128)(2,1)S(1)}, u32[]{:S(2)}, u32[]{:S(2)}) collective-permute-start(bf16[256,512]{0,1:T(8,128)(2,1)S(1)} %collective-permute-done.6), channel_id=1, source_target_pairs={{0,1},{1,2},{2,3},{3,4},{4,5},{5,6},{6,7},{7,8},{8,9},{9,10},{10,1... | collective-permute-start | bytes 786440 | tf_op jit(solution)/shard_map/ppermute | solution.py:30
  179.5 2.5 fusion.24
  182.5 2.7 fusion.64
  185.1 5.6 %fusion.65 = (f32[2048]{0:T(1024)S(1)}, f32[2048,1280]{1,0:T(8,128)}) fusion(bf16[1280,4,128]{0,2,1:T(8,128)(2,1)S(1)} %bitcast.187, bf16[256,4,8,128]{3,2,1,0:T(8,128)(2,1)S(1)} %bitcast.177, pred[256,1280]{1,0:T(8,128)(4,1)S(1)} %compare_and_fusion), kind=kOutput, calls=%fused_computation.122 | convolution fusion | flops 678950912 | bytes 11673600 | tf_op jit(solution)/shard_map/dot_general | solution.py:48
  190.8 5.3 %fusion.66 = (f32[2048]{0:T(1024)S(1)}, f32[2048,1280]{1,0:T(8,128)}) fusion(bf16[1280,4,128]{0,2,1:T(8,128)(2,1)S(1)} %bitcast.188, bf16[256,4,8,128]{3,2,1,0:T(8,128)(2,1)S(1)} %bitcast.178, pred[256,1280]{1,0:T(8,128)(4,1)S(1)} %compare_and_fusion), kind=kOutput, calls=%fused_computation.123 | convolution fusion | flops 678950912 | bytes 11673600 | tf_op jit(solution)/shard_map/dot_general | solution.py:48
  196.1 5.1 %fusion.67 = (f32[2048]{0:T(1024)S(1)}, f32[2048,1280]{1,0:T(8,128)}) fusion(bf16[1280,4,128]{0,2,1:T(8,128)(2,1)S(1)} %bitcast.189, bf16[256,4,8,128]{3,2,1,0:T(8,128)(2,1)S(1)} %bitcast.179, pred[256,1280]{1,0:T(8,128)(4,1)S(1)} %compare_and_fusion), kind=kOutput, calls=%fused_computation.124 | convolution fusion | flops 678950912 | bytes 11673600 | tf_op jit(solution)/shard_map/dot_general | solution.py:48
  201.2 1.8 fusion.6
  203.1 5.7 %fusion.4 = f32[2048]{0:T(1024)S(1)} fusion(f32[2048,1280]{1,0:T(8,128)} %get-tuple-element.126, f32[2048]{0:T(1024)S(1)} %get-tuple-element.125), kind=kLoop, calls=%fused_computation.25 | loop fusion | flops 5240832 | bytes 10502144 | tf_op jit(solution)/shard_map/reduce_sum | solution.py:55
  208.9 6.0 %fusion.58 = bf16[256,1,8,128]{3,2,0,1:T(8,128)(2,1)S(1)} fusion(f32[2048,1280]{1,0:T(8,128)} %copy-done.2, f32[2048]{0:T(1024)S(1)} %get-tuple-element.123, f32[256,8]{1,0:T(8,128)S(1)} %div.49, bf16[1280,4,128]{0,2,1:T(8,128)(2,1)S(1)} %bitcast.199), kind=kOutput, calls=%fused_computation.59 | convolution fusion | flops 676855808 | bytes 11476992 | tf_op jit(solution)/shard_map/dot_general | solution.py:57
  214.9 6.0 %fusion.49 = bf16[256,1,8,128]{3,2,0,1:T(8,128)(2,1)S(1)} fusion(f32[2048,1280]{1,0:T(8,128)} %get-tuple-element.126, f32[2048]{0:T(1024)S(1)} %get-tuple-element.125, f32[256,8]{1,0:T(8,128)S(1)} %div.46, bf16[1280,4,128]{0,2,1:T(8,128)(2,1)S(1)} %bitcast.200), kind=kOutput, calls=%fused_computation.56 | convolution fusion | flops 676855808 | bytes 11476992 | tf_op jit(solution)/shard_map/dot_general | solution.py:57
  220.9 1.8 fusion.2
  222.8 5.8 %fusion.40 = bf16[256,1,8,128]{3,2,0,1:T(8,128)(2,1)S(1)} fusion(f32[2048,1280]{1,0:T(8,128)} %get-tuple-element.128, f32[2048]{0:T(1024)S(1)} %get-tuple-element.127, f32[256,8]{1,0:T(8,128)S(1)} %div.43, bf16[1280,4,128]{0,2,1:T(8,128)(2,1)S(1)} %bitcast.201), kind=kOutput, calls=%fused_computation.53 | convolution fusion | flops 676855808 | bytes 11476992 | tf_op jit(solution)/shard_map/dot_general | solution.py:57
  228.6 5.9 %fusion = f32[2048]{0:T(1024)S(1)} fusion(f32[2048,1280]{1,0:T(8,128)} %get-tuple-element.130, f32[2048]{0:T(1024)S(1)} %get-tuple-element.129), kind=kLoop, calls=%fused_computation.21 | loop fusion | flops 5240832 | bytes 10502144 | tf_op jit(solution)/shard_map/reduce_sum | solution.py:55
  234.7 5.8 %fusion.31 = bf16[256,1,8,128]{3,2,0,1:T(8,128)(2,1)S(1)} fusion(f32[2048,1280]{1,0:T(8,128)} %get-tuple-element.130, f32[2048]{0:T(1024)S(1)} %get-tuple-element.129, f32[256,8]{1,0:T(8,128)S(1)} %div.40, bf16[1280,4,128]{0,2,1:T(8,128)(2,1)S(1)} %bitcast.202), kind=kOutput, calls=%fused_computation.50 | convolution fusion | flops 676855808 | bytes 11476992 | tf_op jit(solution)/shard_map/dot_general | solution.py:57
  242.1 3.0 copy.62
  246.1 2.9 copy.63
  249.0 59.4 %psum.7 = f32[8]{0:T(128)} all-reduce(f32[8]{0:T(128)S(1)} %select_reduce_fusion), channel_id=1, replica_groups=mesh['groups'=2,'dp'=16] {'dp'}, use_global_device_ids=true, to_apply=%region_13.16 | all-reduce | flops 8 | bytes 64 | tf_op jit(solution)/shard_map/psum | solution.py:150
  (116 shorter events, 34.1 us)
Async XLA Ops:
  0.6 26.4 %copy-start = (bf16[768,512]{1,0:T(8,128)(2,1)S(1)}, bf16[768,512]{1,0:T(8,128)(2,1)}, u32[]{:S(2)}) copy-start(bf16[768,512]{1,0:T(8,128)(2,1)} %param.14) | copy-start | bytes 2359300
  4.5 150.8 %collective-permute-start.14 = (s32[1]{0:T(128)}, s32[1]{0:T(128)}, u32[]{:S(2)}, u32[]{:S(2)}) collective-permute-start(s32[1]{0:T(128)} %add.136), channel_id=1, source_target_pairs={{1,0},{2,1},{3,2},{4,3},{5,4},{6,5},{7,6},{8,7},{9,8},{10,9},{11,1... | collective-permute-start | bytes 20 | tf_op jit(solution)/shard_map/ppermute | solution.py:30
  30.3 50.2 %collective-permute-start.2 = (bf16[256,512]{0,1:T(8,128)(2,1)}, bf16[256,512]{0,1:T(8,128)(2,1)}, u32[]{:S(2)}, u32[]{:S(2)}) collective-permute-start(bf16[256,512]{0,1:T(8,128)(2,1)} %copy.48), channel_id=1, source_target_pairs={{0,1},{1,2},{2,3},{3,4},{4,5},{5,6},{6,7},{7,8},{8,9},{9,10},{10,1... | collective-permute-start | bytes 786440 | tf_op jit(solution)/shard_map/ppermute | solution.py:30
  36.2 29.7 %collective-permute-start.8 = (bf16[256,512]{0,1:T(8,128)(2,1)S(1)}, bf16[256,512]{0,1:T(8,128)(2,1)}, u32[]{:S(2)}, u32[]{:S(2)}) collective-permute-start(bf16[256,512]{0,1:T(8,128)(2,1)S(1)} %copy.52), channel_id=1, source_target_pairs={{0,1},{1,2},{2,3},{3,4},{4,5},{5,6},{6,7},{7,8},{8,9},{9,10},{10,1... | collective-permute-start | bytes 786440 | tf_op jit(solution)/shard_map/ppermute | solution.py:30
  51.3 41.2 %collective-permute-start.3 = (bf16[256,512]{0,1:T(8,128)(2,1)}, bf16[256,512]{0,1:T(8,128)(2,1)}, u32[]{:S(2)}, u32[]{:S(2)}) collective-permute-start(bf16[256,512]{0,1:T(8,128)(2,1)} %copy.50), channel_id=1, source_target_pairs={{1,0},{2,1},{3,2},{4,3},{5,4},{6,5},{7,6},{8,7},{9,8},{10,9},{11,1... | collective-permute-start | bytes 786440 | tf_op jit(solution)/shard_map/ppermute | solution.py:30
  53.4 13.8 %collective-permute-start.9 = (bf16[256,512]{0,1:T(8,128)(2,1)}, bf16[256,512]{0,1:T(8,128)(2,1)}, u32[]{:S(2)}, u32[]{:S(2)}) collective-permute-start(bf16[256,512]{0,1:T(8,128)(2,1)} %copy.54), channel_id=1, source_target_pairs={{1,0},{2,1},{3,2},{4,3},{5,4},{6,5},{7,6},{8,7},{9,8},{10,9},{11,1... | collective-permute-start | bytes 786440 | tf_op jit(solution)/shard_map/ppermute | solution.py:30
  65.9 113.2 %collective-permute-start.1 = (bf16[256,4096]{1,0:T(8,128)(2,1)}, bf16[256,4096]{1,0:T(8,128)(2,1)}, u32[]{:S(2)}, u32[]{:S(2)}) collective-permute-start(bf16[256,4096]{1,0:T(8,128)(2,1)} %bitcast.184), channel_id=1, source_target_pairs={{1,0},{2,1},{3,2},{4,3},{5,4},{6,5},{7,6},{8,7},{9,8},{10,9},{11,1... | collective-permute-start | bytes 6291464 | tf_op jit(solution)/shard_map/ppermute | solution.py:30
  68.3 30.2 %collective-permute-start.10 = (bf16[256,512]{0,1:T(8,128)(2,1)S(1)}, bf16[256,512]{0,1:T(8,128)(2,1)S(1)}, u32[]{:S(2)}, u32[]{:S(2)}) collective-permute-start(bf16[256,512]{0,1:T(8,128)(2,1)S(1)} %add_add_fusion), channel_id=1, source_target_pairs={{0,1},{1,2},{2,3},{3,4},{4,5},{5,6},{6,7},{7,8},{8,9},{9,10},{10,1... | collective-permute-start | bytes 786440 | tf_op jit(solution)/shard_map/ppermute | solution.py:30
  80.5 98.7 %collective-permute-start = (bf16[256,4096]{1,0:T(8,128)(2,1)}, bf16[256,4096]{1,0:T(8,128)(2,1)}, u32[]{:S(2)}, u32[]{:S(2)}) collective-permute-start(bf16[256,4096]{1,0:T(8,128)(2,1)} %bitcast.185), channel_id=1, source_target_pairs={{0,1},{1,2},{2,3},{3,4},{4,5},{5,6},{6,7},{7,8},{8,9},{9,10},{10,1... | collective-permute-start | bytes 6291464 | tf_op jit(solution)/shard_map/ppermute | solution.py:30
  93.5 53.7 %copy-start.9 = (s32[256]{0:T(256)S(1)}, s32[256]{0:T(256)}, u32[]{:S(2)}) copy-start(s32[256]{0:T(256)} %param.16) | copy-start | bytes 3076
  93.5 17.2 %collective-permute-start.4 = (bf16[256,512]{0,1:T(8,128)(2,1)S(1)}, bf16[256,512]{0,1:T(8,128)(2,1)S(1)}, u32[]{:S(2)}, u32[]{:S(2)}) collective-permute-start(bf16[256,512]{0,1:T(8,128)(2,1)S(1)} %add_add_fusion.1), channel_id=1, source_target_pairs={{0,1},{1,2},{2,3},{3,4},{4,5},{5,6},{6,7},{7,8},{8,9},{9,10},{10,1... | collective-permute-start | bytes 786440 | tf_op jit(solution)/shard_map/ppermute | solution.py:30
  98.5 44.4 %collective-permute-start.11 = (bf16[256,512]{0,1:T(8,128)(2,1)S(1)}, bf16[256,512]{0,1:T(8,128)(2,1)S(1)}, u32[]{:S(2)}, u32[]{:S(2)}) collective-permute-start(bf16[256,512]{0,1:T(8,128)(2,1)S(1)} %collective-permute-done.10), channel_id=1, source_target_pairs={{0,1},{1,2},{2,3},{3,4},{4,5},{5,6},{6,7},{7,8},{8,9},{9,10},{10,1... | collective-permute-start | bytes 786440 | tf_op jit(solution)/shard_map/ppermute | solution.py:30
  110.8 39.7 %copy-start.4 = (bf16[256,512]{0,1:T(8,128)(2,1)}, bf16[256,512]{0,1:T(8,128)(2,1)S(1)}, u32[]{:S(2)}) copy-start(bf16[256,512]{0,1:T(8,128)(2,1)S(1)} %collective-permute-done.4) | copy-start | bytes 786436
  110.8 36.5 %collective-permute-start.5 = (bf16[256,512]{0,1:T(8,128)(2,1)S(1)}, bf16[256,512]{0,1:T(8,128)(2,1)S(1)}, u32[]{:S(2)}, u32[]{:S(2)}) collective-permute-start(bf16[256,512]{0,1:T(8,128)(2,1)S(1)} %collective-permute-done.4), channel_id=1, source_target_pairs={{0,1},{1,2},{2,3},{3,4},{4,5},{5,6},{6,7},{7,8},{8,9},{9,10},{10,1... | collective-permute-start | bytes 786440 | tf_op jit(solution)/shard_map/ppermute | solution.py:30
  142.8 7.7 %copy-start.6 = (bf16[256,512]{0,1:T(8,128)(2,1)}, bf16[256,512]{0,1:T(8,128)(2,1)S(1)}, u32[]{:S(2)}) copy-start(bf16[256,512]{0,1:T(8,128)(2,1)S(1)} %collective-permute-done.11) | copy-start | bytes 786436
  142.9 7.7 %collective-permute-start.12 = (bf16[256,512]{0,1:T(8,128)(2,1)S(1)}, bf16[256,512]{0,1:T(8,128)(2,1)S(1)}, u32[]{:S(2)}, u32[]{:S(2)}) collective-permute-start(bf16[256,512]{0,1:T(8,128)(2,1)S(1)} %collective-permute-done.11), channel_id=1, source_target_pairs={{0,1},{1,2},{2,3},{3,4},{4,5},{5,6},{6,7},{7,8},{8,9},{9,10},{10,1... | collective-permute-start | bytes 786440 | tf_op jit(solution)/shard_map/ppermute | solution.py:30
  147.3 8.8 %collective-permute-start.6 = (bf16[256,512]{0,1:T(8,128)(2,1)S(1)}, bf16[256,512]{0,1:T(8,128)(2,1)S(1)}, u32[]{:S(2)}, u32[]{:S(2)}) collective-permute-start(bf16[256,512]{0,1:T(8,128)(2,1)S(1)} %collective-permute-done.5), channel_id=1, source_target_pairs={{0,1},{1,2},{2,3},{3,4},{4,5},{5,6},{6,7},{7,8},{8,9},{9,10},{10,1... | collective-permute-start | bytes 786440 | tf_op jit(solution)/shard_map/ppermute | solution.py:30
  150.5 27.2 %collective-permute-start.13 = (bf16[256,512]{0,1:T(8,128)(2,1)S(1)}, bf16[256,512]{0,1:T(8,128)(2,1)S(1)}, u32[]{:S(2)}, u32[]{:S(2)}) collective-permute-start(bf16[256,512]{0,1:T(8,128)(2,1)S(1)} %collective-permute-done.12), channel_id=1, source_target_pairs={{0,1},{1,2},{2,3},{3,4},{4,5},{5,6},{6,7},{7,8},{8,9},{9,10},{10,1... | collective-permute-start | bytes 786440 | tf_op jit(solution)/shard_map/ppermute | solution.py:30
  156.1 23.0 %copy-start.5 = (bf16[256,512]{0,1:T(8,128)(2,1)S(1)}, bf16[256,512]{0,1:T(8,128)(2,1)}, u32[]{:S(2)}) copy-start(bf16[256,512]{0,1:T(8,128)(2,1)} %copy-done.4) | copy-start | bytes 786436
  156.1 22.9 %collective-permute-start.7 = (bf16[256,512]{0,1:T(8,128)(2,1)S(1)}, bf16[256,512]{0,1:T(8,128)(2,1)S(1)}, u32[]{:S(2)}, u32[]{:S(2)}) collective-permute-start(bf16[256,512]{0,1:T(8,128)(2,1)S(1)} %collective-permute-done.6), channel_id=1, source_target_pairs={{0,1},{1,2},{2,3},{3,4},{4,5},{5,6},{6,7},{7,8},{8,9},{9,10},{10,1... | collective-permute-start | bytes 786440 | tf_op jit(solution)/shard_map/ppermute | solution.py:30
  177.8 1.7 copy-start.3
  179.0 35.9 %copy-start.7 = (bf16[1280,512]{0,1:T(8,128)(2,1)}, bf16[1280,512]{0,1:T(8,128)(2,1)S(1)}, u32[]{:S(2)}) copy-start(bf16[1280,512]{0,1:T(8,128)(2,1)S(1)} %constant_dynamic-update-slice_fusion.5) | copy-start | bytes 3932164
  185.1 16.1 %copy-start.2 = (f32[2048,1280]{1,0:T(8,128)}, f32[2048,1280]{1,0:T(8,128)S(1)}, u32[]{:S(2)}) copy-start(f32[2048,1280]{1,0:T(8,128)S(1)} %get-tuple-element.124) | copy-start | bytes 31457284
  208.9 12.0 %slice-start = ((s8[10485760]{0:T(1024)(128)(4,1)}), s8[4194304]{0:T(1024)(128)(4,1)S(1)}, s32[]{:S(2)}) async-start(s8[10485760]{0:T(1024)(128)(4,1)} %bitcast.172), calls=%async_computation | async-start | bytes 8388608
  208.9 12.0 %slice-start.1 = ((s8[10485760]{0:T(1024)(128)(4,1)}), s8[4194304]{0:T(1024)(128)(4,1)S(1)}, s32[]{:S(2)}) async-start(s8[10485760]{0:T(1024)(128)(4,1)} %bitcast.172), calls=%async_computation.1 | async-start | bytes 8388608
  214.9 6.0 %slice-start.2 = ((s8[10485760]{0:T(1024)(128)(4,1)}), s8[2097152]{0:T(1024)(128)(4,1)S(1)}, s32[]{:S(2)}) async-start(s8[10485760]{0:T(1024)(128)(4,1)} %bitcast.172), calls=%async_computation.2 | async-start | bytes 4194304
  220.9 1.9 copy-start.8
  242.1 3.0 copy-start.10
  246.0 62.4 %copy-start.1 = (bf16[768,512]{1,0:T(8,128)(2,1)S(1)}, bf16[768,512]{1,0:T(8,128)(2,1)}, u32[]{:S(2)}) copy-start(bf16[768,512]{1,0:T(8,128)(2,1)} %param.14) | copy-start | bytes 2359300
where the time goes:
time: 310 us; the launch traced here: 308 us
  starting transfers between devices  123 us (40%)
  blocking collectives  75.2 us (24%)
  matrix products  43.2 us (14%)
  local copies, waits for them, and re-layouts  34.3 us (11%)
  other arithmetic  29.4 us (9%)
  between operations  3.36 us (1%)
    ppermute x15, starting transfers between devices, shifted(): return lax.ppermute(block, axis, route)  123 us
    psum x1, blocking collectives, shards(): rewards = lax.psum(partial_rewards, 'dp')  59.4 us
    dot_general x4, matrix products, attend(): jnp.dot(soft_weights, value_heads[:, head_index], preferred_element_type=...  23.6 us
    dot_general x4, matrix products, attend(): jnp.dot(query_head, key_heads[:, head_index].T, preferred_element_type=jn...  18.7 us
    gather x9, local copies, waits for them, and re-layouts, outgoing(): chosen = jnp.take(blocks, bounded, axis=0)  17.2 us
    unnamed x1, blocking collectives  15.8 us
    reduce_sum x4, other arithmetic, attend(): totals = jnp.sum(raised, axis=-1)  15.1 us
    unnamed x45, local copies, waits for them, and re-layouts  8.63 us
  transfers between devices with their start and end apart: 15, of which 0 were waited for; matrix products, arithmetic and copies ran while one was open for 11% of the time, Pallas kernels for 0%

commit v1 on v0

--- a/solution.py
+++ b/solution.py
@@ -147,7 +147,9 @@
         segment_ids[:, None] == jnp.arange(response_count, dtype=jnp.int32)[None, :]
     ) & is_last[:, None]
     partial_rewards = jnp.sum(jnp.where(matches, token_score[:, None], 0.0), axis=0)
-    rewards = lax.psum(partial_rewards, "dp")
+    rewards = partial_rewards
+    for hop_ in (1, 2, 4, 8):
+        rewards = rewards + lax.ppermute(rewards, "dp", [(dev, dev ^ hop_) for dev in range(16)])
     return (attn_out, rewards)
 
 

time: 310 us -> 293 us (0.945)
  blocking collectives: 75.2 us -> 15.8 us
  starting transfers between devices: 123 us -> 159 us
  waiting for transfers between devices: 0.04 us -> 5.49 us
    psum x1 -> x0, blocking collectives: 59.4 us -> none  [shards(): rewards = lax.psum(partial_rewards, 'dp')]
    ppermute x0 -> x4, starting transfers between devices: none -> 36.7 us  [shards(): lax.ppermute(rewards, 'dp', [(dev, dev ^ hop_) for dev in range(16)])]
    ppermute x0 -> x4, waiting for transfers between devices: none -> 5.46 us  [shards(): lax.ppermute(rewards, 'dp', [(dev, dev ^ hop_) for dev in range(16)])]
  transfers between devices with their start and end apart: 15 -> 19, of which waited for: 0 -> 4; matrix products, arithmetic and copies ran while one was open for 11% -> 12% of each run, Pallas kernels for 0% -> 0%
where the time goes in v1:
time: 293 us; the launch traced here: 291 us
  starting transfers between devices  159 us (54%)
  matrix products  43.2 us (15%)
  local copies, waits for them, and re-layouts  34.4 us (12%)
  other arithmetic  30 us (10%)
  blocking collectives  15.8 us (5%)
  waiting for transfers between devices  5.49 us (2%)
  between operations  3.3 us (1%)
    ppermute x15, starting transfers between devices, shifted(): return lax.ppermute(block, axis, route)  122 us
    ppermute x4, starting transfers between devices, shards(): lax.ppermute(rewards, 'dp', [(dev, dev ^ hop_) for dev in range(16)])  36.7 us
    dot_general x4, matrix products, attend(): jnp.dot(soft_weights, value_heads[:, head_index], preferred_element_type=...  23.6 us
    dot_general x4, matrix products, attend(): jnp.dot(query_head, key_heads[:, head_index].T, preferred_element_type=jn...  18.7 us
    gather x9, local copies, waits for them, and re-layouts, outgoing(): chosen = jnp.take(blocks, bounded, axis=0)  17.2 us
    unnamed x1, blocking collectives  15.8 us
    reduce_sum x4, other arithmetic, attend(): totals = jnp.sum(raised, axis=-1)  15.1 us
    unnamed x45, local copies, waits for them, and re-layouts  8.68 us
  transfers between devices with their start and end apart: 19, of which 4 were waited for; matrix products, arithmetic and copies ran while one was open for 12% of the time, Pallas kernels for 0%

profile of v1, /device:TPU:0, one launch (start us, length us, event | category | flops | bytes accessed | tf_op | source)
XLA Modules:
  0.0 291.2 jit_solution(7640645194891241703)
XLA Ops:
  11.2 15.8 %all-reduce.4 = (s32[16]{0:T(128)S(1)}, s32[16]{0:T(128)S(1)}, s32[16]{0:T(128)S(1)}, s32[16]{0:T(128)S(1)}) all-reduce(s32[16]{0:T(128)S(1)} %dynamic-update-slice, s32[16]{0:T(128)S(1)} %slice_dynamic-update-slice_fusion, s32[16]{0:T(128)S(1)} %get-tuple-element.116, ...), channel_id=2, replica_groups=mesh['groups'=2,'dp'=16] {'dp'}, use_global_device_ids=true, to_apply=%add | all-reduce | flops 64 | bytes 512
  30.4 5.8 %collective-permute-start.2 = (bf16[256,512]{0,1:T(8,128)(2,1)}, bf16[256,512]{0,1:T(8,128)(2,1)}, u32[]{:S(2)}, u32[]{:S(2)}) collective-permute-start(bf16[256,512]{0,1:T(8,128)(2,1)} %copy.48), channel_id=1, source_target_pairs={{0,1},{1,2},{2,3},{3,4},{4,5},{5,6},{6,7},{7,8},{8,9},{9,10},{10,1... | collective-permute-start | bytes 786440 | tf_op jit(solution)/shard_map/ppermute | solution.py:30
  36.3 11.7 %collective-permute-start.8 = (bf16[256,512]{0,1:T(8,128)(2,1)S(1)}, bf16[256,512]{0,1:T(8,128)(2,1)}, u32[]{:S(2)}, u32[]{:S(2)}) collective-permute-start(bf16[256,512]{0,1:T(8,128)(2,1)S(1)} %copy.52), channel_id=1, source_target_pairs={{0,1},{1,2},{2,3},{3,4},{4,5},{5,6},{6,7},{7,8},{8,9},{9,10},{10,1... | collective-permute-start | bytes 786440 | tf_op jit(solution)/shard_map/ppermute | solution.py:30
  54.7 3.5 %gather_fusion.2 = bf16[2,128,4096]{2,1,0:T(8,128)(2,1)S(1)} fusion(bf16[6,128,4096]{2,1,0:T(8,128)(2,1)} %bitcast.181, s32[1024]{0:T(1024)S(1)} %get-tuple-element.133), kind=kCustom, calls=%fused_computation.3.clone | custom fusion | bytes 4194312 | tf_op jit(solution)/shard_map/jit(_take)/gather | solution.py:114
  62.1 3.5 %gather_fusion.1 = bf16[2,128,4096]{2,1,0:T(8,128)(2,1)S(1)} fusion(bf16[6,128,4096]{2,1,0:T(8,128)(2,1)} %bitcast.182, s32[1024]{0:T(1024)S(1)} %get-tuple-element.134), kind=kCustom, calls=%fused_computation.2.clone | custom fusion | bytes 4194312 | tf_op jit(solution)/shard_map/jit(_take)/gather | solution.py:114
  68.3 6.9 %collective-permute-start.10 = (bf16[256,512]{0,1:T(8,128)(2,1)S(1)}, bf16[256,512]{0,1:T(8,128)(2,1)S(1)}, u32[]{:S(2)}, u32[]{:S(2)}) collective-permute-start(bf16[256,512]{0,1:T(8,128)(2,1)S(1)} %add_add_fusion), channel_id=1, source_target_pairs={{0,1},{1,2},{2,3},{3,4},{4,5},{5,6},{6,7},{7,8},{8,9},{9,10},{10,1... | collective-permute-start | bytes 786440 | tf_op jit(solution)/shard_map/ppermute | solution.py:30
  76.8 3.5 %gather_fusion = bf16[2,128,4096]{2,1,0:T(8,128)(2,1)S(1)} fusion(bf16[6,128,4096]{2,1,0:T(8,128)(2,1)} %bitcast.183, s32[1024]{0:T(1024)S(1)} %pad_clamp_fusion.2), kind=kCustom, calls=%fused_computation.clone | custom fusion | bytes 4194312 | tf_op jit(solution)/shard_map/jit(_take)/gather | solution.py:114
  80.4 12.0 %collective-permute-start = (bf16[256,4096]{1,0:T(8,128)(2,1)}, bf16[256,4096]{1,0:T(8,128)(2,1)}, u32[]{:S(2)}, u32[]{:S(2)}) collective-permute-start(bf16[256,4096]{1,0:T(8,128)(2,1)} %bitcast.185), channel_id=1, source_target_pairs={{0,1},{1,2},{2,3},{3,4},{4,5},{5,6},{6,7},{7,8},{8,9},{9,10},{10,1... | collective-permute-start | bytes 6291464 | tf_op jit(solution)/shard_map/ppermute | solution.py:30
  93.5 4.8 %collective-permute-start.4 = (bf16[256,512]{0,1:T(8,128)(2,1)S(1)}, bf16[256,512]{0,1:T(8,128)(2,1)S(1)}, u32[]{:S(2)}, u32[]{:S(2)}) collective-permute-start(bf16[256,512]{0,1:T(8,128)(2,1)S(1)} %add_add_fusion.1), channel_id=1, source_target_pairs={{0,1},{1,2},{2,3},{3,4},{4,5},{5,6},{6,7},{7,8},{8,9},{9,10},{10,1... | collective-permute-start | bytes 786440 | tf_op jit(solution)/shard_map/ppermute | solution.py:30
  98.3 10.6 %collective-permute-start.11 = (bf16[256,512]{0,1:T(8,128)(2,1)S(1)}, bf16[256,512]{0,1:T(8,128)(2,1)S(1)}, u32[]{:S(2)}, u32[]{:S(2)}) collective-permute-start(bf16[256,512]{0,1:T(8,128)(2,1)S(1)} %collective-permute-done.10), channel_id=1, source_target_pairs={{0,1},{1,2},{2,3},{3,4},{4,5},{5,6},{6,7},{7,8},{8,9},{9,10},{10,1... | collective-permute-start | bytes 786440 | tf_op jit(solution)/shard_map/ppermute | solution.py:30
  110.6 32.0 %collective-permute-start.5 = (bf16[256,512]{0,1:T(8,128)(2,1)S(1)}, bf16[256,512]{0,1:T(8,128)(2,1)S(1)}, u32[]{:S(2)}, u32[]{:S(2)}) collective-permute-start(bf16[256,512]{0,1:T(8,128)(2,1)S(1)} %collective-permute-done.4), channel_id=1, source_target_pairs={{0,1},{1,2},{2,3},{3,4},{4,5},{5,6},{6,7},{7,8},{8,9},{9,10},{10,1... | collective-permute-start | bytes 786440 | tf_op jit(solution)/shard_map/ppermute | solution.py:30
  142.7 4.4 %collective-permute-start.12 = (bf16[256,512]{0,1:T(8,128)(2,1)S(1)}, bf16[256,512]{0,1:T(8,128)(2,1)S(1)}, u32[]{:S(2)}, u32[]{:S(2)}) collective-permute-start(bf16[256,512]{0,1:T(8,128)(2,1)S(1)} %collective-permute-done.11), channel_id=1, source_target_pairs={{0,1},{1,2},{2,3},{3,4},{4,5},{5,6},{6,7},{7,8},{8,9},{9,10},{10,1... | collective-permute-start | bytes 786440 | tf_op jit(solution)/shard_map/ppermute | solution.py:30
  147.1 3.2 %collective-permute-start.6 = (bf16[256,512]{0,1:T(8,128)(2,1)S(1)}, bf16[256,512]{0,1:T(8,128)(2,1)S(1)}, u32[]{:S(2)}, u32[]{:S(2)}) collective-permute-start(bf16[256,512]{0,1:T(8,128)(2,1)S(1)} %collective-permute-done.5), channel_id=1, source_target_pairs={{0,1},{1,2},{2,3},{3,4},{4,5},{5,6},{6,7},{7,8},{8,9},{9,10},{10,1... | collective-permute-start | bytes 786440 | tf_op jit(solution)/shard_map/ppermute | solution.py:30
  150.4 4.4 %collective-permute-start.13 = (bf16[256,512]{0,1:T(8,128)(2,1)S(1)}, bf16[256,512]{0,1:T(8,128)(2,1)S(1)}, u32[]{:S(2)}, u32[]{:S(2)}) collective-permute-start(bf16[256,512]{0,1:T(8,128)(2,1)S(1)} %collective-permute-done.12), channel_id=1, source_target_pairs={{0,1},{1,2},{2,3},{3,4},{4,5},{5,6},{6,7},{7,8},{8,9},{9,10},{10,1... | collective-permute-start | bytes 786440 | tf_op jit(solution)/shard_map/ppermute | solution.py:30
  155.9 21.4 %collective-permute-start.7 = (bf16[256,512]{0,1:T(8,128)(2,1)S(1)}, bf16[256,512]{0,1:T(8,128)(2,1)S(1)}, u32[]{:S(2)}, u32[]{:S(2)}) collective-permute-start(bf16[256,512]{0,1:T(8,128)(2,1)S(1)} %collective-permute-done.6), channel_id=1, source_target_pairs={{0,1},{1,2},{2,3},{3,4},{4,5},{5,6},{6,7},{7,8},{8,9},{9,10},{10,1... | collective-permute-start | bytes 786440 | tf_op jit(solution)/shard_map/ppermute | solution.py:30
  179.0 2.5 fusion.24
  182.1 2.7 fusion.64
  184.7 5.6 %fusion.65 = (f32[2048]{0:T(1024)S(1)}, f32[2048,1280]{1,0:T(8,128)}) fusion(bf16[1280,4,128]{0,2,1:T(8,128)(2,1)S(1)} %bitcast.187, bf16[256,4,8,128]{3,2,1,0:T(8,128)(2,1)S(1)} %bitcast.177, pred[256,1280]{1,0:T(8,128)(4,1)S(1)} %compare_and_fusion), kind=kOutput, calls=%fused_computation.122 | convolution fusion | flops 678950912 | bytes 11673600 | tf_op jit(solution)/shard_map/dot_general | solution.py:48
  190.3 5.3 %fusion.66 = (f32[2048]{0:T(1024)S(1)}, f32[2048,1280]{1,0:T(8,128)}) fusion(bf16[1280,4,128]{0,2,1:T(8,128)(2,1)S(1)} %bitcast.188, bf16[256,4,8,128]{3,2,1,0:T(8,128)(2,1)S(1)} %bitcast.178, pred[256,1280]{1,0:T(8,128)(4,1)S(1)} %compare_and_fusion), kind=kOutput, calls=%fused_computation.123 | convolution fusion | flops 678950912 | bytes 11673600 | tf_op jit(solution)/shard_map/dot_general | solution.py:48
  195.6 5.1 %fusion.67 = (f32[2048]{0:T(1024)S(1)}, f32[2048,1280]{1,0:T(8,128)}) fusion(bf16[1280,4,128]{0,2,1:T(8,128)(2,1)S(1)} %bitcast.189, bf16[256,4,8,128]{3,2,1,0:T(8,128)(2,1)S(1)} %bitcast.179, pred[256,1280]{1,0:T(8,128)(4,1)S(1)} %compare_and_fusion), kind=kOutput, calls=%fused_computation.124 | convolution fusion | flops 678950912 | bytes 11673600 | tf_op jit(solution)/shard_map/dot_general | solution.py:48
  202.7 5.7 %fusion.4 = f32[2048]{0:T(1024)S(1)} fusion(f32[2048,1280]{1,0:T(8,128)} %get-tuple-element.126, f32[2048]{0:T(1024)S(1)} %get-tuple-element.125), kind=kLoop, calls=%fused_computation.25 | loop fusion | flops 5240832 | bytes 10502144 | tf_op jit(solution)/shard_map/reduce_sum | solution.py:55
  208.5 6.0 %fusion.58 = bf16[256,1,8,128]{3,2,0,1:T(8,128)(2,1)S(1)} fusion(f32[2048,1280]{1,0:T(8,128)} %copy-done.2, f32[2048]{0:T(1024)S(1)} %get-tuple-element.123, f32[256,8]{1,0:T(8,128)S(1)} %div.49, bf16[1280,4,128]{0,2,1:T(8,128)(2,1)S(1)} %bitcast.199), kind=kOutput, calls=%fused_computation.59 | convolution fusion | flops 676855808 | bytes 11476992 | tf_op jit(solution)/shard_map/dot_general | solution.py:57
  214.5 6.0 %fusion.49 = bf16[256,1,8,128]{3,2,0,1:T(8,128)(2,1)S(1)} fusion(f32[2048,1280]{1,0:T(8,128)} %get-tuple-element.126, f32[2048]{0:T(1024)S(1)} %get-tuple-element.125, f32[256,8]{1,0:T(8,128)S(1)} %div.46, bf16[1280,4,128]{0,2,1:T(8,128)(2,1)S(1)} %bitcast.200), kind=kOutput, calls=%fused_computation.56 | convolution fusion | flops 676855808 | bytes 11476992 | tf_op jit(solution)/shard_map/dot_general | solution.py:57
  222.4 5.8 %fusion.40 = bf16[256,1,8,128]{3,2,0,1:T(8,128)(2,1)S(1)} fusion(f32[2048,1280]{1,0:T(8,128)} %get-tuple-element.128, f32[2048]{0:T(1024)S(1)} %get-tuple-element.127, f32[256,8]{1,0:T(8,128)S(1)} %div.43, bf16[1280,4,128]{0,2,1:T(8,128)(2,1)S(1)} %bitcast.201), kind=kOutput, calls=%fused_computation.53 | convolution fusion | flops 676855808 | bytes 11476992 | tf_op jit(solution)/shard_map/dot_general | solution.py:57
  228.2 5.9 %fusion = f32[2048]{0:T(1024)S(1)} fusion(f32[2048,1280]{1,0:T(8,128)} %get-tuple-element.130, f32[2048]{0:T(1024)S(1)} %get-tuple-element.129), kind=kLoop, calls=%fused_computation.21 | loop fusion | flops 5240832 | bytes 10502144 | tf_op jit(solution)/shard_map/reduce_sum | solution.py:55
  234.2 5.8 %fusion.31 = bf16[256,1,8,128]{3,2,0,1:T(8,128)(2,1)S(1)} fusion(f32[2048,1280]{1,0:T(8,128)} %get-tuple-element.130, f32[2048]{0:T(1024)S(1)} %get-tuple-element.129, f32[256,8]{1,0:T(8,128)S(1)} %div.40, bf16[1280,4,128]{0,2,1:T(8,128)(2,1)S(1)} %bitcast.202), kind=kOutput, calls=%fused_computation.50 | convolution fusion | flops 676855808 | bytes 11476992 | tf_op jit(solution)/shard_map/dot_general | solution.py:57
  241.6 3.0 %copy.62 = bf16[256,4,8,128]{0,3,2,1:T(8,128)(2,1)S(1)} copy(bf16[256,4,8,128]{3,2,0,1:T(8,128)(2,1)} %pad_maximum_fusion) | data formatting | bytes 4194304 | tf_op jit(solution)/shard_map/stack | solution.py:62
  244.6 2.9 copy.63
  248.6 4.1 %collective-permute-start.15 = (f32[8]{0:T(128)S(1)}, f32[8]{0:T(128)S(1)}, u32[]{:S(2)}, u32[]{:S(2)}) collective-permute-start(f32[8]{0:T(128)S(1)} %select_reduce_fusion), channel_id=1, source_target_pairs={{0,1},{1,0},{2,3},{3,2},{4,5},{5,4},{6,7},{7,6},{8,9},{9,8},{10,11... | collective-permute-start | bytes 104 | tf_op jit(solution)/shard_map/ppermute | solution.py:152
  253.5 3.7 %collective-permute-start.16 = (f32[8]{0:T(128)S(1)}, f32[8]{0:T(128)S(1)}, u32[]{:S(2)}, u32[]{:S(2)}) collective-permute-start(f32[8]{0:T(128)S(1)} %add.147), channel_id=1, source_target_pairs={{0,2},{1,3},{2,0},{3,1},{4,6},{5,7},{6,4},{7,5},{8,10},{9,11},{10,... | collective-permute-start | bytes 104 | tf_op jit(solution)/shard_map/ppermute | solution.py:152
  258.7 23.3 %collective-permute-start.17 = (f32[8]{0:T(128)S(1)}, f32[8]{0:T(128)S(1)}, u32[]{:S(2)}, u32[]{:S(2)}) collective-permute-start(f32[8]{0:T(128)S(1)} %add.148), channel_id=1, source_target_pairs={{0,4},{1,5},{2,6},{3,7},{4,0},{5,1},{6,2},{7,3},{8,12},{9,13},{10,... | collective-permute-start | bytes 104 | tf_op jit(solution)/shard_map/ppermute | solution.py:152
  283.6 5.6 %collective-permute-start.18 = (f32[8]{0:T(128)S(1)}, f32[8]{0:T(128)S(1)}, u32[]{:S(2)}, u32[]{:S(2)}) collective-permute-start(f32[8]{0:T(128)S(1)} %add.149), channel_id=1, source_target_pairs={{0,8},{1,9},{2,10},{3,11},{4,12},{5,13},{6,14},{7,15},{8,0},{9,1},... | collective-permute-start | bytes 104 | tf_op jit(solution)/shard_map/ppermute | solution.py:152
  (127 shorter events, 45.6 us)
Async XLA Ops:
  0.6 26.5 %copy-start = (bf16[768,512]{1,0:T(8,128)(2,1)S(1)}, bf16[768,512]{1,0:T(8,128)(2,1)}, u32[]{:S(2)}) copy-start(bf16[768,512]{1,0:T(8,128)(2,1)} %param.14) | copy-start | bytes 2359300
  4.6 150.6 %collective-permute-start.14 = (s32[1]{0:T(128)}, s32[1]{0:T(128)}, u32[]{:S(2)}, u32[]{:S(2)}) collective-permute-start(s32[1]{0:T(128)} %add.146), channel_id=1, source_target_pairs={{1,0},{2,1},{3,2},{4,3},{5,4},{6,5},{7,6},{8,7},{9,8},{10,9},{11,1... | collective-permute-start | bytes 20 | tf_op jit(solution)/shard_map/ppermute | solution.py:30
  30.4 50.0 %collective-permute-start.2 = (bf16[256,512]{0,1:T(8,128)(2,1)}, bf16[256,512]{0,1:T(8,128)(2,1)}, u32[]{:S(2)}, u32[]{:S(2)}) collective-permute-start(bf16[256,512]{0,1:T(8,128)(2,1)} %copy.48), channel_id=1, source_target_pairs={{0,1},{1,2},{2,3},{3,4},{4,5},{5,6},{6,7},{7,8},{8,9},{9,10},{10,1... | collective-permute-start | bytes 786440 | tf_op jit(solution)/shard_map/ppermute | solution.py:30
  36.3 29.5 %collective-permute-start.8 = (bf16[256,512]{0,1:T(8,128)(2,1)S(1)}, bf16[256,512]{0,1:T(8,128)(2,1)}, u32[]{:S(2)}, u32[]{:S(2)}) collective-permute-start(bf16[256,512]{0,1:T(8,128)(2,1)S(1)} %copy.52), channel_id=1, source_target_pairs={{0,1},{1,2},{2,3},{3,4},{4,5},{5,6},{6,7},{7,8},{8,9},{9,10},{10,1... | collective-permute-start | bytes 786440 | tf_op jit(solution)/shard_map/ppermute | solution.py:30
  51.3 41.1 %collective-permute-start.3 = (bf16[256,512]{0,1:T(8,128)(2,1)}, bf16[256,512]{0,1:T(8,128)(2,1)}, u32[]{:S(2)}, u32[]{:S(2)}) collective-permute-start(bf16[256,512]{0,1:T(8,128)(2,1)} %copy.50), channel_id=1, source_target_pairs={{1,0},{2,1},{3,2},{4,3},{5,4},{6,5},{7,6},{8,7},{9,8},{10,9},{11,1... | collective-permute-start | bytes 786440 | tf_op jit(solution)/shard_map/ppermute | solution.py:30
  53.4 13.8 %collective-permute-start.9 = (bf16[256,512]{0,1:T(8,128)(2,1)}, bf16[256,512]{0,1:T(8,128)(2,1)}, u32[]{:S(2)}, u32[]{:S(2)}) collective-permute-start(bf16[256,512]{0,1:T(8,128)(2,1)} %copy.54), channel_id=1, source_target_pairs={{1,0},{2,1},{3,2},{4,3},{5,4},{6,5},{7,6},{8,7},{9,8},{10,9},{11,1... | collective-permute-start | bytes 786440 | tf_op jit(solution)/shard_map/ppermute | solution.py:30
  65.9 112.8 %collective-permute-start.1 = (bf16[256,4096]{1,0:T(8,128)(2,1)}, bf16[256,4096]{1,0:T(8,128)(2,1)}, u32[]{:S(2)}, u32[]{:S(2)}) collective-permute-start(bf16[256,4096]{1,0:T(8,128)(2,1)} %bitcast.184), channel_id=1, source_target_pairs={{1,0},{2,1},{3,2},{4,3},{5,4},{6,5},{7,6},{8,7},{9,8},{10,9},{11,1... | collective-permute-start | bytes 6291464 | tf_op jit(solution)/shard_map/ppermute | solution.py:30
  68.3 30.0 %collective-permute-start.10 = (bf16[256,512]{0,1:T(8,128)(2,1)S(1)}, bf16[256,512]{0,1:T(8,128)(2,1)S(1)}, u32[]{:S(2)}, u32[]{:S(2)}) collective-permute-start(bf16[256,512]{0,1:T(8,128)(2,1)S(1)} %add_add_fusion), channel_id=1, source_target_pairs={{0,1},{1,2},{2,3},{3,4},{4,5},{5,6},{6,7},{7,8},{8,9},{9,10},{10,1... | collective-permute-start | bytes 786440 | tf_op jit(solution)/shard_map/ppermute | solution.py:30
  80.4 98.3 %collective-permute-start = (bf16[256,4096]{1,0:T(8,128)(2,1)}, bf16[256,4096]{1,0:T(8,128)(2,1)}, u32[]{:S(2)}, u32[]{:S(2)}) collective-permute-start(bf16[256,4096]{1,0:T(8,128)(2,1)} %bitcast.185), channel_id=1, source_target_pairs={{0,1},{1,2},{2,3},{3,4},{4,5},{5,6},{6,7},{7,8},{8,9},{9,10},{10,1... | collective-permute-start | bytes 6291464 | tf_op jit(solution)/shard_map/ppermute | solution.py:30
  93.5 53.6 %copy-start.9 = (s32[256]{0:T(256)S(1)}, s32[256]{0:T(256)}, u32[]{:S(2)}) copy-start(s32[256]{0:T(256)} %param.16) | copy-start | bytes 3076
  93.5 17.2 %collective-permute-start.4 = (bf16[256,512]{0,1:T(8,128)(2,1)S(1)}, bf16[256,512]{0,1:T(8,128)(2,1)S(1)}, u32[]{:S(2)}, u32[]{:S(2)}) collective-permute-start(bf16[256,512]{0,1:T(8,128)(2,1)S(1)} %add_add_fusion.1), channel_id=1, source_target_pairs={{0,1},{1,2},{2,3},{3,4},{4,5},{5,6},{6,7},{7,8},{8,9},{9,10},{10,1... | collective-permute-start | bytes 786440 | tf_op jit(solution)/shard_map/ppermute | solution.py:30
  98.3 44.3 %collective-permute-start.11 = (bf16[256,512]{0,1:T(8,128)(2,1)S(1)}, bf16[256,512]{0,1:T(8,128)(2,1)S(1)}, u32[]{:S(2)}, u32[]{:S(2)}) collective-permute-start(bf16[256,512]{0,1:T(8,128)(2,1)S(1)} %collective-permute-done.10), channel_id=1, source_target_pairs={{0,1},{1,2},{2,3},{3,4},{4,5},{5,6},{6,7},{7,8},{8,9},{9,10},{10,1... | collective-permute-start | bytes 786440 | tf_op jit(solution)/shard_map/ppermute | solution.py:30
  110.6 39.7 %copy-start.4 = (bf16[256,512]{0,1:T(8,128)(2,1)}, bf16[256,512]{0,1:T(8,128)(2,1)S(1)}, u32[]{:S(2)}) copy-start(bf16[256,512]{0,1:T(8,128)(2,1)S(1)} %collective-permute-done.4) | copy-start | bytes 786436
  110.6 36.5 %collective-permute-start.5 = (bf16[256,512]{0,1:T(8,128)(2,1)S(1)}, bf16[256,512]{0,1:T(8,128)(2,1)S(1)}, u32[]{:S(2)}, u32[]{:S(2)}) collective-permute-start(bf16[256,512]{0,1:T(8,128)(2,1)S(1)} %collective-permute-done.4), channel_id=1, source_target_pairs={{0,1},{1,2},{2,3},{3,4},{4,5},{5,6},{6,7},{7,8},{8,9},{9,10},{10,1... | collective-permute-start | bytes 786440 | tf_op jit(solution)/shard_map/ppermute | solution.py:30
  142.7 7.7 %copy-start.6 = (bf16[256,512]{0,1:T(8,128)(2,1)}, bf16[256,512]{0,1:T(8,128)(2,1)S(1)}, u32[]{:S(2)}) copy-start(bf16[256,512]{0,1:T(8,128)(2,1)S(1)} %collective-permute-done.11) | copy-start | bytes 786436
  142.7 7.7 %collective-permute-start.12 = (bf16[256,512]{0,1:T(8,128)(2,1)S(1)}, bf16[256,512]{0,1:T(8,128)(2,1)S(1)}, u32[]{:S(2)}, u32[]{:S(2)}) collective-permute-start(bf16[256,512]{0,1:T(8,128)(2,1)S(1)} %collective-permute-done.11), channel_id=1, source_target_pairs={{0,1},{1,2},{2,3},{3,4},{4,5},{5,6},{6,7},{7,8},{8,9},{9,10},{10,1... | collective-permute-start | bytes 786440 | tf_op jit(solution)/shard_map/ppermute | solution.py:30
  147.1 8.8 %collective-permute-start.6 = (bf16[256,512]{0,1:T(8,128)(2,1)S(1)}, bf16[256,512]{0,1:T(8,128)(2,1)S(1)}, u32[]{:S(2)}, u32[]{:S(2)}) collective-permute-start(bf16[256,512]{0,1:T(8,128)(2,1)S(1)} %collective-permute-done.5), channel_id=1, source_target_pairs={{0,1},{1,2},{2,3},{3,4},{4,5},{5,6},{6,7},{7,8},{8,9},{9,10},{10,1... | collective-permute-start | bytes 786440 | tf_op jit(solution)/shard_map/ppermute | solution.py:30
  150.4 26.9 %collective-permute-start.13 = (bf16[256,512]{0,1:T(8,128)(2,1)S(1)}, bf16[256,512]{0,1:T(8,128)(2,1)S(1)}, u32[]{:S(2)}, u32[]{:S(2)}) collective-permute-start(bf16[256,512]{0,1:T(8,128)(2,1)S(1)} %collective-permute-done.12), channel_id=1, source_target_pairs={{0,1},{1,2},{2,3},{3,4},{4,5},{5,6},{6,7},{7,8},{8,9},{9,10},{10,1... | collective-permute-start | bytes 786440 | tf_op jit(solution)/shard_map/ppermute | solution.py:30
  155.9 22.8 %copy-start.5 = (bf16[256,512]{0,1:T(8,128)(2,1)S(1)}, bf16[256,512]{0,1:T(8,128)(2,1)}, u32[]{:S(2)}) copy-start(bf16[256,512]{0,1:T(8,128)(2,1)} %copy-done.4) | copy-start | bytes 786436
  155.9 22.7 %collective-permute-start.7 = (bf16[256,512]{0,1:T(8,128)(2,1)S(1)}, bf16[256,512]{0,1:T(8,128)(2,1)S(1)}, u32[]{:S(2)}, u32[]{:S(2)}) collective-permute-start(bf16[256,512]{0,1:T(8,128)(2,1)S(1)} %collective-permute-done.6), channel_id=1, source_target_pairs={{0,1},{1,2},{2,3},{3,4},{4,5},{5,6},{6,7},{7,8},{8,9},{9,10},{10,1... | collective-permute-start | bytes 786440 | tf_op jit(solution)/shard_map/ppermute | solution.py:30
  178.6 35.9 %copy-start.7 = (bf16[1280,512]{0,1:T(8,128)(2,1)}, bf16[1280,512]{0,1:T(8,128)(2,1)S(1)}, u32[]{:S(2)}) copy-start(bf16[1280,512]{0,1:T(8,128)(2,1)S(1)} %constant_dynamic-update-slice_fusion.5) | copy-start | bytes 3932164
  184.7 16.1 %copy-start.2 = (f32[2048,1280]{1,0:T(8,128)}, f32[2048,1280]{1,0:T(8,128)S(1)}, u32[]{:S(2)}) copy-start(f32[2048,1280]{1,0:T(8,128)S(1)} %get-tuple-element.124) | copy-start | bytes 31457284
  208.4 12.0 %slice-start = ((s8[10485760]{0:T(1024)(128)(4,1)}), s8[4194304]{0:T(1024)(128)(4,1)S(1)}, s32[]{:S(2)}) async-start(s8[10485760]{0:T(1024)(128)(4,1)} %bitcast.172), calls=%async_computation | async-start | bytes 8388608
  208.5 12.0 %slice-start.1 = ((s8[10485760]{0:T(1024)(128)(4,1)}), s8[4194304]{0:T(1024)(128)(4,1)S(1)}, s32[]{:S(2)}) async-start(s8[10485760]{0:T(1024)(128)(4,1)} %bitcast.172), calls=%async_computation.1 | async-start | bytes 8388608
  214.4 6.0 %slice-start.2 = ((s8[10485760]{0:T(1024)(128)(4,1)}), s8[2097152]{0:T(1024)(128)(4,1)S(1)}, s32[]{:S(2)}) async-start(s8[10485760]{0:T(1024)(128)(4,1)} %bitcast.172), calls=%async_computation.2 | async-start | bytes 4194304
  220.5 1.9 copy-start.8
  244.6 2.9 copy-start.10
  244.6 46.6 %copy-start.1 = (bf16[768,512]{1,0:T(8,128)(2,1)S(1)}, bf16[768,512]{1,0:T(8,128)(2,1)}, u32[]{:S(2)}) copy-start(bf16[768,512]{1,0:T(8,128)(2,1)} %param.14) | copy-start | bytes 2359300
  248.6 4.9 %collective-permute-start.15 = (f32[8]{0:T(128)S(1)}, f32[8]{0:T(128)S(1)}, u32[]{:S(2)}, u32[]{:S(2)}) collective-permute-start(f32[8]{0:T(128)S(1)} %select_reduce_fusion), channel_id=1, source_target_pairs={{0,1},{1,0},{2,3},{3,2},{4,5},{5,4},{6,7},{7,6},{8,9},{9,8},{10,11... | collective-permute-start | bytes 104 | tf_op jit(solution)/shard_map/ppermute | solution.py:152
  253.5 5.2 %collective-permute-start.16 = (f32[8]{0:T(128)S(1)}, f32[8]{0:T(128)S(1)}, u32[]{:S(2)}, u32[]{:S(2)}) collective-permute-start(f32[8]{0:T(128)S(1)} %add.147), channel_id=1, source_target_pairs={{0,2},{1,3},{2,0},{3,1},{4,6},{5,7},{6,4},{7,5},{8,10},{9,11},{10,... | collective-permute-start | bytes 104 | tf_op jit(solution)/shard_map/ppermute | solution.py:152
  258.7 24.8 %collective-permute-start.17 = (f32[8]{0:T(128)S(1)}, f32[8]{0:T(128)S(1)}, u32[]{:S(2)}, u32[]{:S(2)}) collective-permute-start(f32[8]{0:T(128)S(1)} %add.148), channel_id=1, source_target_pairs={{0,4},{1,5},{2,6},{3,7},{4,0},{5,1},{6,2},{7,3},{8,12},{9,13},{10,... | collective-permute-start | bytes 104 | tf_op jit(solution)/shard_map/ppermute | solution.py:152
  283.6 7.2 %collective-permute-start.18 = (f32[8]{0:T(128)S(1)}, f32[8]{0:T(128)S(1)}, u32[]{:S(2)}, u32[]{:S(2)}) collective-permute-start(f32[8]{0:T(128)S(1)} %add.149), channel_id=1, source_target_pairs={{0,8},{1,9},{2,10},{3,11},{4,12},{5,13},{6,14},{7,15},{8,0},{9,1},... | collective-permute-start | bytes 104 | tf_op jit(solution)/shard_map/ppermute | solution.py:152
  (1 other events, 1.7 us)
